TPU v7x, 32 devices: a whole 2x2x4 slice. The times are simulated.
32 devices in a mesh: blk: 16 (over z, y, core), tensor: 2 (over x).
Axes of the slice: x: 2, y: 2, z: 4, core: 2. Of those that a mesh axis runs over, the one named last changes fastest.
Arguments:
- tokens: bfloat16 [64, 8192], P('blk'), may hold values from -6 to 6
- gate_weight: bfloat16 [29568, 8192], P(('blk', 'tensor')), may hold values from -0.0625 to 0.0625
- up_weight: bfloat16 [29568, 8192], P(('blk', 'tensor')), may hold values from -0.0625 to 0.0625
- down_weight: bfloat16 [29568, 8192], P(('blk', 'tensor')), may hold values from -0.03125 to 0.03125
Outputs:
- mixed: bfloat16 [64, 8192], P(('blk', 'tensor'))
All inputs are finite; a program needn't handle non-finite values.
Results may differ from a plain program's by a relative error of at most 0.009.
Values may be sent and summed in bfloat16 or wider, within the bound.
A program may use at most 128 MiB of HBM per device.

v0:
```python
import jax
import jax.numpy as jnp
from jax import lax
from jax.sharding import PartitionSpec as P


def project_rows(left, weight):
    return lax.dot_general(
        left, weight, (((1,), (1,)), ((), ())), preferred_element_type=jnp.float32
    )


def per_device(tokens, gate_weight, up_weight, down_weight):
    piece = lax.all_gather(tokens, "blk", axis=0, tiled=True)
    gate = project_rows(piece, gate_weight)
    up_part = project_rows(piece, up_weight)
    hidden = (jax.nn.silu(gate) * up_part).astype(jnp.bfloat16)
    total = lax.psum_scatter(
        jnp.dot(hidden, down_weight, preferred_element_type=jnp.float32),
        ("blk", "tensor"),
        scatter_dimension=0,
        tiled=True,
    )
    return total.astype(jnp.bfloat16)


def solution(mesh):
    placed = (
        P("blk", None),
        P(("blk", "tensor"), None),
        P(("blk", "tensor"), None),
        P(("blk", "tensor"), None),
    )
    return jax.shard_map(
        per_device,
        mesh=mesh,
        in_specs=placed,
        out_specs=P(("blk", "tensor"), None),
        check_vma=False,
    )
```

profile of v0, /device:TPU:0, one launch (start us, length us, event | category | flops | bytes accessed | tf_op | source)
XLA Modules:
  0.0 145.2 jit_solution(6302948357680619052)
XLA Ops:
  6.5 0.0 all-gather.3.cloned.1.call-start
  6.5 0.7 all-gather.3.cloned.1.call-update
  7.3 42.9 %all-gather.3.cloned.1.call-done = bf16[16,4,8192]{2,1,0:T(4,128)(2,1)} async-done(((bf16[1,4,8192]{2,1,0:T(4,128)(2,1)}), bf16[16,4,8192]{2,1,0:T(4,128)(2,1)}) %all-gather.3.cloned.1.call-update) | async-done | bytes 1048592 | tf_op jit(solution)/shard_map/all_gather | solution.py:14
  50.1 1.3 reshape.1
  51.5 9.9 %fusion.9 = f32[64,924]{1,0:T(8,128)S(1)} fusion(bf16[64,8192]{1,0:T(8,128)(2,1)S(1)} %reshape.1, bf16[924,8192]{1,0:T(8,128)(2,1)} %param.5), kind=kOutput, calls=%fused_computation.11 | convolution fusion | flops 968884224 | bytes 16423936 | tf_op jit(solution)/shard_map/dot_general | solution.py:8
  61.4 14.4 %fusion.1 = f32[64,8192]{1,0:T(8,128)S(1)} fusion(bf16[924,8192]{1,0:T(8,128)(2,1)} %param.7, bf16[64,8192]{1,0:T(8,128)(2,1)S(1)} %reshape.1, bf16[924,8192]{1,0:T(8,128)(2,1)} %param.6, f32[64,924]{1,0:T(8,128)S(1)} %fusion.9), kind=kOutput, calls=%fused_computation.2 | convolution fusion | flops 1938123264 | bytes 33659904 | tf_op jit(solution)/shard_map/dot_general | solution.py:19
  75.8 61.9 %all-reduce.2 = bf16[64,8192]{1,0:T(8,128)(2,1)S(1)} all-reduce(f32[64,8192]{1,0:T(8,128)S(1)} %fusion.1), channel_id=2, replica_groups=mesh['blk'=16,'tensor'=2] {'blk','tensor'}, use_global_device_ids=true, to_apply=%region_0.1.clone | all-reduce | flops 524288 | bytes 3145728
  137.7 0.7 dynamic-slice_convert_fusion
Async XLA Ops:
  6.5 43.6 %all-gather.3.cloned.1.call-start = ((), (), s32[]{:S(2)}) async-start(), calls=%async_computation | async-start | bytes 1114112 | tf_op jit(solution)/shard_map/all_gather | solution.py:14
Sparse Core Ops, SparseCore 0:
  9.5 40.5 all-gather.2
where the time goes:
time: 145 us
  blocking collectives  61.9 us (43%)
  waiting for transfers between devices  43.6 us (30%)
  matrix products  24.3 us (17%)
  between operations  13.4 us (9%)
  local copies, waits for them, and re-layouts  1.99 us (1%)
    unnamed x1, blocking collectives  61.9 us
    all_gather x1, waiting for transfers between devices, per_device(): piece = lax.all_gather(tokens, 'blk', axis=0, tiled=True)  42.9 us
    dot_general x1, matrix products, per_device(): jnp.dot(hidden, down_weight, preferred_element_type=jnp.float32)  14.4 us
    dot_general x1, matrix products, project_rows(): lax.dot_general(left, weight, (((1,), (1,)), ((), ())), preferred_element...  9.94 us
  transfers between devices with their start and end apart: 1, of which 1 were waited for; matrix products, arithmetic and copies ran while one was open for 0% of the time, Pallas kernels for 0%

commit v1 on v0

v1 whole, which is shorter than its diff:
```python
import functools

import jax
import jax.numpy as jnp
from jax import lax
from jax.experimental import pallas as pl
from jax.experimental.pallas import tpu as pltpu
from jax.sharding import PartitionSpec as P

MESH = pl.DeviceIdType.MESH
CHUNKS = 4
TILE = 512


def kernel(
    chips, tensors,
    tok, wg, wu, wd, out,
    wgv, wuv, wdv, gathered, x2d, gacc, uacc, hid, own, part, near, stage, far,
    tok_sem, w_sem, ag_send, ag_recv, fw_send, fw_recv, near_send, near_recv, far_send, far_recv,
):
    blk, ten = lax.axis_index("blk"), lax.axis_index("tensor")
    core, chip = lax.rem(blk, 2), lax.div(blk, 2)
    other = 1 - core
    mate = (chip * 2 + other, ten)
    owners = chips * tensors
    me = chip * tensors + ten
    width = tok.shape[1] // CHUNKS
    rows = tok.shape[0]
    share = rows // tensors

    def owner_of(step):
        index = lax.rem(me + step, owners)
        return index, (lax.div(index, tensors) * 2 + core, lax.rem(index, tensors))

    def cols(k):
        return pl.ds(k * width, width)

    def tok_copy(k):
        return pltpu.make_async_copy(tok.at[:, cols(k)], gathered.at[k, core, chip], tok_sem.at[k])

    def w_copy(which, k):
        src, dst = ((wg, wgv), (wu, wuv), (wd, wdv))[which]
        return pltpu.make_async_copy(src.at[:, cols(k)], dst.at[k], w_sem.at[which, k])

    for k in range(CHUNKS):
        tok_copy(k).start()
    for k in range(CHUNKS):
        w_copy(0, k).start()
        w_copy(1, k).start()

    barrier = pltpu.get_barrier_semaphore()
    pl.semaphore_signal(barrier, inc=1, device_id=mate, device_id_type=MESH)

    @pl.loop(1, owners)
    def _(step):
        pl.semaphore_signal(barrier, inc=1, device_id=owner_of(step)[1], device_id_type=MESH)

    pl.semaphore_wait(barrier, owners)

    def ag_copy(k, step, slot):
        to = lax.rem(chip + step, chips)
        return pltpu.make_async_remote_copy(
            src_ref=gathered.at[k, core, slot], dst_ref=gathered.at[k, core, slot],
            send_sem=ag_send.at[k, to], recv_sem=ag_recv.at[k, slot],
            device_id=(to * 2 + core, ten), device_id_type=MESH,
        )

    def fw_copy(k, side):
        return pltpu.make_async_remote_copy(
            src_ref=gathered.at[k, side], dst_ref=gathered.at[k, side],
            send_sem=fw_send.at[k], recv_sem=fw_recv.at[k],
            device_id=mate, device_id_type=MESH,
        )

    for k in range(CHUNKS):
        tok_copy(k).wait()

        @pl.loop(1, chips)
        def _(step):
            ag_copy(k, step, chip).start()

    for k in range(CHUNKS):
        w_copy(2, k).start()

    def forward(k):
        @pl.loop(1, chips)
        def _(step):
            ag_copy(k, step, lax.rem(chip + step, chips)).wait_recv()

        fw_copy(k, core).start()

    gacc[...] = jnp.zeros_like(gacc)
    uacc[...] = jnp.zeros_like(uacc)

    def project(k, start, stop):
        @pl.loop(start, stop)
        def _(step):
            at = pl.ds(pl.multiple_of(step * TILE, TILE), TILE)
            for side in range(2):
                for c in range(chips):
                    low = (side * chips + c) * rows
                    x2d[low:low + rows, :] = gathered[k, side, c, :, at]
            x = x2d[...]
            dims = (((1,), (1,)), ((), ()))
            gacc[...] += lax.dot_general(x, wgv[k, :, at], dims, preferred_element_type=jnp.float32)
            uacc[...] += lax.dot_general(x, wuv[k, :, at], dims, preferred_element_type=jnp.float32)

    tiles = width // TILE
    forward(0)
    for k in range(CHUNKS):
        fw_copy(k, other).wait_recv()
        w_copy(0, k).wait()
        w_copy(1, k).wait()
        project(k, 0, tiles // 2)
        if k + 1 < CHUNKS:
            forward(k + 1)
        project(k, tiles // 2, tiles)

    gate = gacc[...]
    hid[...] = (gate / (1.0 + jnp.exp(-gate)) * uacc[...]).astype(hid.dtype)

    def near_copy(j):
        return pltpu.make_async_remote_copy(
            src_ref=part.at[j, other], dst_ref=near.at[j],
            send_sem=near_send.at[j], recv_sem=near_recv.at[j],
            device_id=mate, device_id_type=MESH,
        )

    def far_copy(j, step, slot):
        to, device = owner_of(step)
        return pltpu.make_async_remote_copy(
            src_ref=stage.at[j, to], dst_ref=far.at[j, slot],
            send_sem=far_send.at[j, to], recv_sem=far_recv.at[j, slot],
            device_id=device, device_id_type=MESH,
        )

    half = chips * rows

    def down(j):
        w_copy(2, j).wait()

        @pl.loop(0, tiles)
        def _(step):
            at = pl.ds(pl.multiple_of(step * TILE, TILE), TILE)
            p = jnp.dot(hid[...], wdv[j, :, at], preferred_element_type=jnp.float32)
            for side in range(2):
                piece = p[side * half:(side + 1) * half]
                own[j, side, :, at] = piece
                part[j, side, :, at] = piece.astype(part.dtype)

        near_copy(j).start()

    def send_far(j):
        near_copy(j).wait_recv()

        @pl.loop(0, tiles)
        def _(step):
            at = pl.ds(pl.multiple_of(step * TILE, TILE), TILE)
            s = own[j, core, :, at] + near[j, :, at].astype(jnp.float32)
            for d in range(owners):
                stage[j, d, :, at] = s[d * share:(d + 1) * share].astype(stage.dtype)

        @pl.loop(1, owners)
        def _(step):
            far_copy(j, step, me).start()

    for j in range(CHUNKS):
        down(j)
        if j:
            send_far(j - 1)
    send_far(CHUNKS - 1)

    for j in range(CHUNKS):
        @pl.loop(1, owners)
        def _(step):
            far_copy(j, step, lax.rem(me + step, owners)).wait_recv()

        def add(step, acc):
            return acc + far[j, lax.rem(me + step, owners)].astype(jnp.float32)

        total = lax.fori_loop(1, owners, add, stage[j, me].astype(jnp.float32))
        out[:, j * width:(j + 1) * width] = total.astype(out.dtype)

    for k in range(CHUNKS):
        @pl.loop(1, chips)
        def _(step):
            ag_copy(k, step, chip).wait_send()

        @pl.loop(1, owners)
        def _(step):
            far_copy(k, step, me).wait_send()

        fw_copy(k, core).wait_send()
        near_copy(k).wait_send()


def per_device(blks, tensors, tokens, gate_weight, up_weight, down_weight):
    rows, depth = tokens.shape
    units = gate_weight.shape[0]
    chips, width = blks // 2, depth // CHUNKS
    owners, share = chips * tensors, rows // tensors
    everyone, half = blks * rows, chips * rows
    bf, f32, dma = jnp.bfloat16, jnp.float32, pltpu.SemaphoreType.DMA
    anywhere = pl.BlockSpec(memory_space=pl.ANY)
    return pl.pallas_call(
        functools.partial(kernel, chips, tensors),
        out_shape=jax.ShapeDtypeStruct((share, depth), bf),
        in_specs=[anywhere] * 4,
        out_specs=pl.BlockSpec(memory_space=pltpu.VMEM),
        scratch_shapes=[
            pltpu.VMEM((CHUNKS, units, width), bf),
            pltpu.VMEM((CHUNKS, units, width), bf),
            pltpu.VMEM((CHUNKS, units, width), bf),
            pltpu.VMEM((CHUNKS, 2, chips, rows, width), bf),
            pltpu.VMEM((everyone, TILE), bf),
            pltpu.VMEM((everyone, units), f32),
            pltpu.VMEM((everyone, units), f32),
            pltpu.VMEM((everyone, units), bf),
            pltpu.VMEM((CHUNKS, 2, half, width), f32),
            pltpu.VMEM((CHUNKS, 2, half, width), bf),
            pltpu.VMEM((CHUNKS, half, width), bf),
            pltpu.VMEM((CHUNKS, owners, share, width), bf),
            pltpu.VMEM((CHUNKS, owners, share, width), bf),
            dma((CHUNKS,)),
            dma((3, CHUNKS)),
            dma((CHUNKS, chips)),
            dma((CHUNKS, chips)),
            dma((CHUNKS,)),
            dma((CHUNKS,)),
            dma((CHUNKS,)),
            dma((CHUNKS,)),
            dma((CHUNKS, owners)),
            dma((CHUNKS, owners)),
        ],
        compiler_params=pltpu.CompilerParams(
            collective_id=0, has_side_effects=True, vmem_limit_bytes=60 * 1024 * 1024
        ),
    )(tokens, gate_weight, up_weight, down_weight)


def solution(mesh):
    placed = (
        P("blk", None),
        P(("blk", "tensor"), None),
        P(("blk", "tensor"), None),
        P(("blk", "tensor"), None),
    )
    return jax.shard_map(
        functools.partial(per_device, mesh.shape["blk"], mesh.shape["tensor"]),
        mesh=mesh,
        in_specs=placed,
        out_specs=P(("blk", "tensor"), None),
        check_vma=False,
    )
```

time: 145 us -> 49.4 us (0.34)
  blocking collectives: 61.9 us -> 0 us
  Pallas kernels: 0 us -> 47.8 us
  waiting for transfers between devices: 43.6 us -> 0 us
  matrix products: 24.3 us -> 0 us
  between operations: 13.4 us -> 0.01 us
    unnamed x1 -> x0, blocking collectives: 61.9 us -> none
    pallas_call x0 -> x1, Pallas kernels: none -> 47.8 us  [per_device(): pl.pallas_call(functools.partial(kernel, chips, tensors), out_shape=jax.S...]
    all_gather x1 -> x0, waiting for transfers between devices: 42.9 us -> none  [per_device(): piece = lax.all_gather(tokens, 'blk', axis=0, tiled=True)]
    dot_general x2 -> x0, matrix products: 24.3 us -> none  [the longest x1 14.4 us: per_device(): jnp.dot(hidden, down_weight, preferred_element_type=jnp.float32)]
  transfers between devices with their start and end apart: 1 -> 0, of which waited for: 1 -> 0; matrix products, arithmetic and copies ran while one was open for 0% -> 0% of each run, Pallas kernels for 0% -> 0%
where the time goes in v1:
time: 49.4 us; the launch traced here: 49.2 us
  Pallas kernels  47.8 us (97%)
  local copies, waits for them, and re-layouts  1.4 us (3%)
    pallas_call x1, Pallas kernels, per_device(): pl.pallas_call(functools.partial(kernel, chips, tensors), out_shape=jax.S...  47.8 us
    unnamed x1, local copies, waits for them, and re-layouts  1.4 us

profile of v1, /device:TPU:0, one launch (start us, length us, event | category | flops | bytes accessed | tf_op | source)
XLA Modules:
  0.0 49.2 jit_solution(4288626955335741952)
XLA Ops:
  0.0 47.8 %shard_map.46 = bf16[2,8192]{1,0:T(2,128)(2,1)} custom-call(bf16[4,8192]{1,0:T(4,128)(2,1)} %tok.1, bf16[924,8192]{1,0:T(8,128)(2,1)} %wg.1, bf16[924,8192]{1,0:T(8,128)(2,1)} %wu.1, bf16[924,8192]{1,0:T(8,128)(2,1)} %wd.1), custom_call_target="tpu_custom_call" | custom-call | tf_op jit(solution)/shard_map/pallas_call | solution.py:205
  47.8 1.4 %copy.6 = bf16[2,8192]{1,0:T(2,128)(2,1)} copy(bf16[2,8192]{1,0:T(2,128)(2,1)} %shard_map.46) | data formatting | bytes 65536

commit v2 on v1

v2 whole, which is shorter than its diff:
```python
import functools

import jax
import jax.numpy as jnp
from jax import lax
from jax.experimental import pallas as pl
from jax.experimental.pallas import tpu as pltpu
from jax.sharding import PartitionSpec as P

MESH = pl.DeviceIdType.MESH
CHUNKS = 4
TILE = 512


def kernel(
    outers, inners, tensors,
    tok, wg, wu, wd, out,
    wgv, wuv, wdv, gathered, x2d, gacc, uacc, hid, own, part, near, stage, mid, held, far,
    tok_sem, w_sem, ag_send, ag_recv, in_send, in_recv, fw_send, fw_recv,
    near_send, near_recv, mid_send, mid_recv, far_send, far_recv,
):
    blk, ten = lax.axis_index("blk"), lax.axis_index("tensor")
    core, chip = lax.rem(blk, 2), lax.div(blk, 2)
    outer, inner = lax.div(chip, inners), lax.rem(chip, inners)
    other = 1 - core
    mate = (blk + 1 - 2 * core, ten)
    planes = inners * tensors
    plane = inner * tensors + ten
    width = tok.shape[1] // CHUNKS
    rows = tok.shape[0]
    share = rows // tensors

    def outer_peer(step):
        to = lax.rem(outer + step, outers)
        return to, ((to * inners + inner) * 2 + core, ten)

    def inner_peer(step):
        to = lax.rem(inner + step, inners)
        return to, ((outer * inners + to) * 2 + core, ten)

    def plane_peer(step):
        to = lax.rem(plane + step, planes)
        return to, ((outer * inners + lax.div(to, tensors)) * 2 + core, lax.rem(to, tensors))

    def cols(k):
        return pl.ds(k * width, width)

    def tok_copy(k):
        return pltpu.make_async_copy(tok.at[:, cols(k)], gathered.at[k, core, inner, outer], tok_sem.at[k])

    def w_copy(which, k):
        src, dst = ((wg, wgv), (wu, wuv), (wd, wdv))[which]
        return pltpu.make_async_copy(src.at[:, cols(k)], dst.at[k], w_sem.at[which, k])

    for k in range(CHUNKS):
        tok_copy(k).start()
    for k in range(CHUNKS):
        w_copy(0, k).start()
        w_copy(1, k).start()

    barrier = pltpu.get_barrier_semaphore()
    pl.semaphore_signal(barrier, inc=1, device_id=mate, device_id_type=MESH)

    for step in range(1, planes):
        pl.semaphore_signal(barrier, inc=1, device_id=plane_peer(step)[1], device_id_type=MESH)
    for step in range(1, outers):
        pl.semaphore_signal(barrier, inc=1, device_id=outer_peer(step)[1], device_id_type=MESH)
    pl.semaphore_wait(barrier, planes + outers - 1)

    def ag_copy(k, step, slot):
        to, device = outer_peer(step)
        block = gathered.at[k, core, inner, slot]
        return pltpu.make_async_remote_copy(
            src_ref=block, dst_ref=block,
            send_sem=ag_send.at[k, to], recv_sem=ag_recv.at[k, slot],
            device_id=device, device_id_type=MESH,
        )

    def in_copy(k, step, slot):
        to, device = inner_peer(step)
        block = gathered.at[k, core, slot]
        return pltpu.make_async_remote_copy(
            src_ref=block, dst_ref=block,
            send_sem=in_send.at[k, to], recv_sem=in_recv.at[k, slot],
            device_id=device, device_id_type=MESH,
        )

    def fw_copy(k, side, slot):
        block = gathered.at[k, side, slot]
        return pltpu.make_async_remote_copy(
            src_ref=block, dst_ref=block,
            send_sem=fw_send.at[k, slot], recv_sem=fw_recv.at[k, slot],
            device_id=mate, device_id_type=MESH,
        )

    for k in range(CHUNKS):
        tok_copy(k).wait()

        for step in range(1, outers):
            ag_copy(k, step, outer).start()

    for k in range(CHUNKS):
        w_copy(2, k).start()

    def forward(k):
        for step in range(1, outers):
            ag_copy(k, step, outer_peer(step)[0]).wait_recv()
        for step in range(1, inners):
            in_copy(k, step, inner).start()
        fw_copy(k, core, inner).start()

    def hand_over(k):
        for step in range(1, inners):
            slot = inner_peer(step)[0]
            in_copy(k, step, slot).wait_recv()
            fw_copy(k, core, slot).start()

    gacc[...] = jnp.zeros_like(gacc)
    uacc[...] = jnp.zeros_like(uacc)

    def project(k, start, stop):
        @pl.loop(start, stop)
        def _(step):
            at = pl.ds(pl.multiple_of(step * TILE, TILE), TILE)
            for side in range(2):
                for i in range(inners):
                    for o in range(outers):
                        low = ((side * inners + i) * outers + o) * rows
                        x2d[low:low + rows, :] = gathered[k, side, i, o, :, at]
            x = x2d[...]
            dims = (((1,), (1,)), ((), ()))
            gacc[...] += lax.dot_general(x, wgv[k, :, at], dims, preferred_element_type=jnp.float32)
            uacc[...] += lax.dot_general(x, wuv[k, :, at], dims, preferred_element_type=jnp.float32)

    tiles = width // TILE
    forward(0)
    for k in range(CHUNKS):
        if k + 1 < CHUNKS and k:
            forward(k + 1)
        if not k:
            hand_over(0)
            forward(1)
        for i in range(inners):
            fw_copy(k, other, i).wait_recv()
        w_copy(0, k).wait()
        w_copy(1, k).wait()
        project(k, 0, tiles // 2)
        if k + 1 < CHUNKS:
            hand_over(k + 1)
        project(k, tiles // 2, tiles)

    gate = gacc[...]
    hid[...] = (gate / (1.0 + jnp.exp(-gate)) * uacc[...]).astype(hid.dtype)

    def near_copy(j):
        return pltpu.make_async_remote_copy(
            src_ref=part.at[j, other], dst_ref=near.at[j],
            send_sem=near_send.at[j], recv_sem=near_recv.at[j],
            device_id=mate, device_id_type=MESH,
        )

    def mid_copy(j, step, slot):
        to, device = plane_peer(step)
        return pltpu.make_async_remote_copy(
            src_ref=stage.at[j, to], dst_ref=mid.at[j, slot],
            send_sem=mid_send.at[j, to], recv_sem=mid_recv.at[j, slot],
            device_id=device, device_id_type=MESH,
        )

    def far_copy(j, step, slot):
        to, device = outer_peer(step)
        return pltpu.make_async_remote_copy(
            src_ref=held.at[j, to], dst_ref=far.at[j, slot],
            send_sem=far_send.at[j, to], recv_sem=far_recv.at[j, slot],
            device_id=device, device_id_type=MESH,
        )

    half = inners * outers * rows

    def down(j):
        w_copy(2, j).wait()

        @pl.loop(0, tiles)
        def _(step):
            at = pl.ds(pl.multiple_of(step * TILE, TILE), TILE)
            p = jnp.dot(hid[...], wdv[j, :, at], preferred_element_type=jnp.float32)
            for side in range(2):
                piece = p[side * half:(side + 1) * half]
                own[j, side, :, at] = piece
                part[j, side, :, at] = piece.astype(part.dtype)

        near_copy(j).start()

    def send_mid(j):
        near_copy(j).wait_recv()

        @pl.loop(0, tiles)
        def _(step):
            at = pl.ds(pl.multiple_of(step * TILE, TILE), TILE)
            s = own[j, core, :, at] + near[j, :, at].astype(jnp.float32)
            for i in range(inners):
                for o in range(outers):
                    for t in range(tensors):
                        low = ((i * outers + o) * tensors + t) * share
                        stage[j, i * tensors + t, o, :, at] = s[low:low + share].astype(stage.dtype)

        for step in range(1, planes):
            mid_copy(j, step, plane).start()

    def send_far(j):
        for step in range(1, planes):
            mid_copy(j, step, plane_peer(step)[0]).wait_recv()
        for o in range(outers):
            total = stage[j, plane, o].astype(jnp.float32)
            for step in range(1, planes):
                total += mid[j, plane_peer(step)[0], o].astype(jnp.float32)
            held[j, o] = total.astype(held.dtype)
        for step in range(1, outers):
            far_copy(j, step, outer).start()

    def finish(j):
        total = held[j, outer].astype(jnp.float32)
        for step in range(1, outers):
            slot = outer_peer(step)[0]
            far_copy(j, step, slot).wait_recv()
            total += far[j, slot].astype(jnp.float32)
        out[:, j * width:(j + 1) * width] = total.astype(out.dtype)

    for j in range(CHUNKS):
        down(j)
        if j:
            send_mid(j - 1)
    send_mid(CHUNKS - 1)
    for j in range(CHUNKS):
        send_far(j)
    for j in range(CHUNKS):
        finish(j)

    for k in range(CHUNKS):
        for step in range(1, outers):
            ag_copy(k, step, outer).wait_send()
            far_copy(k, step, outer).wait_send()
        for step in range(1, inners):
            in_copy(k, step, inner).wait_send()
        for step in range(1, planes):
            mid_copy(k, step, plane).wait_send()
        for i in range(inners):
            fw_copy(k, core, i).wait_send()
        near_copy(k).wait_send()


def per_device(blks, tensors, tokens, gate_weight, up_weight, down_weight):
    rows, depth = tokens.shape
    units = gate_weight.shape[0]
    chips, width = blks // 2, depth // CHUNKS
    inners = 2 if chips % 2 == 0 else 1
    outers, planes, share = chips // inners, inners * tensors, rows // tensors
    everyone, half = blks * rows, chips * rows
    bf, f32, dma = jnp.bfloat16, jnp.float32, pltpu.SemaphoreType.DMA
    anywhere = pl.BlockSpec(memory_space=pl.ANY)
    return pl.pallas_call(
        functools.partial(kernel, outers, inners, tensors),
        out_shape=jax.ShapeDtypeStruct((share, depth), bf),
        in_specs=[anywhere] * 4,
        out_specs=pl.BlockSpec(memory_space=pltpu.VMEM),
        scratch_shapes=[
            pltpu.VMEM((CHUNKS, units, width), bf),
            pltpu.VMEM((CHUNKS, units, width), bf),
            pltpu.VMEM((CHUNKS, units, width), bf),
            pltpu.VMEM((CHUNKS, 2, inners, outers, rows, width), bf),
            pltpu.VMEM((everyone, TILE), bf),
            pltpu.VMEM((everyone, units), f32),
            pltpu.VMEM((everyone, units), f32),
            pltpu.VMEM((everyone, units), bf),
            pltpu.VMEM((CHUNKS, 2, half, width), f32),
            pltpu.VMEM((CHUNKS, 2, half, width), bf),
            pltpu.VMEM((CHUNKS, half, width), bf),
            pltpu.VMEM((CHUNKS, planes, outers, share, width), bf),
            pltpu.VMEM((CHUNKS, planes, outers, share, width), bf),
            pltpu.VMEM((CHUNKS, outers, share, width), bf),
            pltpu.VMEM((CHUNKS, outers, share, width), bf),
            dma((CHUNKS,)),
            dma((3, CHUNKS)),
            dma((CHUNKS, outers)),
            dma((CHUNKS, outers)),
            dma((CHUNKS, inners)),
            dma((CHUNKS, inners)),
            dma((CHUNKS, inners)),
            dma((CHUNKS, inners)),
            dma((CHUNKS,)),
            dma((CHUNKS,)),
            dma((CHUNKS, planes)),
            dma((CHUNKS, planes)),
            dma((CHUNKS, outers)),
            dma((CHUNKS, outers)),
        ],
        compiler_params=pltpu.CompilerParams(
            collective_id=0, has_side_effects=True, vmem_limit_bytes=60 * 1024 * 1024
        ),
    )(tokens, gate_weight, up_weight, down_weight)


def solution(mesh):
    placed = (
        P("blk", None),
        P(("blk", "tensor"), None),
        P(("blk", "tensor"), None),
        P(("blk", "tensor"), None),
    )
    return jax.shard_map(
        functools.partial(per_device, mesh.shape["blk"], mesh.shape["tensor"]),
        mesh=mesh,
        in_specs=placed,
        out_specs=P(("blk", "tensor"), None),
        check_vma=False,
    )
```

time: 49.4 us -> 51.8 us (1.049)
  Pallas kernels: 47.8 us -> 50.2 us
    pallas_call x1, Pallas kernels: 47.8 us -> 50.2 us  [per_device(): pl.pallas_call(functools.partial(kernel, outers, inners, tensors), out_sh...]
where the time goes in v2:
time: 51.8 us; the launch traced here: 51.7 us
  Pallas kernels  50.2 us (97%)
  local copies, waits for them, and re-layouts  1.4 us (3%)
    pallas_call x1, Pallas kernels, per_device(): pl.pallas_call(functools.partial(kernel, outers, inners, tensors), out_sh...  50.2 us
    unnamed x1, local copies, waits for them, and re-layouts  1.4 us

profile of v2, /device:TPU:0, one launch (start us, length us, event | category | flops | bytes accessed | tf_op | source)
XLA Modules:
  0.0 51.7 jit_solution(16625869508333679216)
XLA Ops:
  0.0 50.2 %shard_map.46 = bf16[2,8192]{1,0:T(2,128)(2,1)} custom-call(bf16[4,8192]{1,0:T(4,128)(2,1)} %tok.1, bf16[924,8192]{1,0:T(8,128)(2,1)} %wg.1, bf16[924,8192]{1,0:T(8,128)(2,1)} %wu.1, bf16[924,8192]{1,0:T(8,128)(2,1)} %wd.1), custom_call_target="tpu_custom_call" | custom-call | tf_op jit(solution)/shard_map/pallas_call | solution.py:261
  50.3 1.4 %copy.6 = bf16[2,8192]{1,0:T(2,128)(2,1)} copy(bf16[2,8192]{1,0:T(2,128)(2,1)} %shard_map.46) | data formatting | bytes 65536

commit v3 on v2

--- a/solution.py
+++ b/solution.py
@@ -118,39 +118,39 @@
     gacc[...] = jnp.zeros_like(gacc)
     uacc[...] = jnp.zeros_like(uacc)
 
-    def project(k, start, stop):
-        @pl.loop(start, stop)
-        def _(step):
-            at = pl.ds(pl.multiple_of(step * TILE, TILE), TILE)
-            for side in range(2):
-                for i in range(inners):
-                    for o in range(outers):
-                        low = ((side * inners + i) * outers + o) * rows
-                        x2d[low:low + rows, :] = gathered[k, side, i, o, :, at]
-            x = x2d[...]
-            dims = (((1,), (1,)), ((), ()))
-            gacc[...] += lax.dot_general(x, wgv[k, :, at], dims, preferred_element_type=jnp.float32)
-            uacc[...] += lax.dot_general(x, wuv[k, :, at], dims, preferred_element_type=jnp.float32)
+    def collect(k):
+        for i in range(inners):
+            fw_copy(k, other, i).wait_recv()
+        for side in range(2):
+            for i in range(inners):
+                for o in range(outers):
+                    low = ((side * inners + i) * outers + o) * rows
+                    x2d[low:low + rows, :] = gathered[k, side, i, o]
+        w_copy(0, k).wait()
+        w_copy(1, k).wait()
+
+    def project(k, weight, acc):
+        acc[...] += lax.dot_general(
+            weight[k], x2d[...], (((1,), (1,)), ((), ())), preferred_element_type=jnp.float32
+        )
 
     tiles = width // TILE
     forward(0)
-    for k in range(CHUNKS):
-        if k + 1 < CHUNKS and k:
-            forward(k + 1)
-        if not k:
-            hand_over(0)
-            forward(1)
-        for i in range(inners):
-            fw_copy(k, other, i).wait_recv()
-        w_copy(0, k).wait()
-        w_copy(1, k).wait()
-        project(k, 0, tiles // 2)
+    forward(1)
+    hand_over(0)
+    forward(2)
+    for k in range(CHUNKS):
+        collect(k)
+        project(k, wgv, gacc)
+        if k == 0:
+            for later in range(3, CHUNKS):
+                forward(later)
         if k + 1 < CHUNKS:
             hand_over(k + 1)
-        project(k, tiles // 2, tiles)
+        project(k, wuv, uacc)
 
     gate = gacc[...]
-    hid[...] = (gate / (1.0 + jnp.exp(-gate)) * uacc[...]).astype(hid.dtype)
+    hid[...] = (gate / (1.0 + jnp.exp(-gate)) * uacc[...]).T.astype(hid.dtype)
 
     def near_copy(j):
         return pltpu.make_async_remote_copy(
@@ -230,11 +230,12 @@
         down(j)
         if j:
             send_mid(j - 1)
+    send_far(0)
     send_mid(CHUNKS - 1)
-    for j in range(CHUNKS):
+    for j in range(1, CHUNKS):
         send_far(j)
-    for j in range(CHUNKS):
-        finish(j)
+        finish(j - 1)
+    finish(CHUNKS - 1)
 
     for k in range(CHUNKS):
         for step in range(1, outers):
@@ -268,9 +269,9 @@
             pltpu.VMEM((CHUNKS, units, width), bf),
             pltpu.VMEM((CHUNKS, units, width), bf),
             pltpu.VMEM((CHUNKS, 2, inners, outers, rows, width), bf),
-            pltpu.VMEM((everyone, TILE), bf),
-            pltpu.VMEM((everyone, units), f32),
-            pltpu.VMEM((everyone, units), f32),
+            pltpu.VMEM((everyone, width), bf),
+            pltpu.VMEM((units, everyone), f32),
+            pltpu.VMEM((units, everyone), f32),
             pltpu.VMEM((everyone, units), bf),
             pltpu.VMEM((CHUNKS, 2, half, width), f32),
             pltpu.VMEM((CHUNKS, 2, half, width), bf),

time: 51.8 us -> 46.7 us (0.902)
  Pallas kernels: 50.2 us -> 45.1 us
    pallas_call x1, Pallas kernels: 50.2 us -> 45.1 us  [per_device(): pl.pallas_call(functools.partial(kernel, outers, inners, tensors), out_sh...]
where the time goes in v3:
time: 46.7 us; the launch traced here: 46.5 us
  Pallas kernels  45.1 us (97%)
  local copies, waits for them, and re-layouts  1.4 us (3%)
    pallas_call x1, Pallas kernels, per_device(): pl.pallas_call(functools.partial(kernel, outers, inners, tensors), out_sh...  45.1 us
    unnamed x1, local copies, waits for them, and re-layouts  1.4 us

profile of v3, /device:TPU:0, one launch (start us, length us, event | category | flops | bytes accessed | tf_op | source)
XLA Modules:
  0.0 46.5 jit_solution(5345475520239799836)
XLA Ops:
  0.0 45.1 %shard_map.46 = bf16[2,8192]{1,0:T(2,128)(2,1)} custom-call(bf16[4,8192]{1,0:T(4,128)(2,1)} %tok.1, bf16[924,8192]{1,0:T(8,128)(2,1)} %wg.1, bf16[924,8192]{1,0:T(8,128)(2,1)} %wu.1, bf16[924,8192]{1,0:T(8,128)(2,1)} %wd.1), custom_call_target="tpu_custom_call" | custom-call | tf_op jit(solution)/shard_map/pallas_call | solution.py:262
  45.1 1.4 %copy.6 = bf16[2,8192]{1,0:T(2,128)(2,1)} copy(bf16[2,8192]{1,0:T(2,128)(2,1)} %shard_map.46) | data formatting | bytes 65536
